TPU v7x, 32 devices: a whole 2x2x4 slice. The times are simulated.
32 devices in a mesh: row: 4 (over y, core), col: 8 (over z, x).
Axes of the slice: x: 2, y: 2, z: 4, core: 2. Of those that a mesh axis runs over, the one named last changes fastest.
Arguments:
- l_saved: bfloat16 [16, 4, 256, 8, 256], P(None, 'row', None, 'col'), as said below
- l_grad: bfloat16 [16, 4, 256, 8, 256], P(None, 'row', None, 'col'), as said below
Outputs:
- grad_out: float32 [16, 4, 256, 8, 256], P(None, 'row', None, 'col')
Inputs may be any that keep to these rules, and one draw needn't show every extreme that they name: Read as one matrix of 16384 rows, l_saved is lower triangular with its diagonal between 1 and 2. Read as one matrix, l_grad is zero above the diagonal.
All inputs are finite; a program needn't handle non-finite values.
Results may differ from a plain program's by a relative error of at most 0.0003.
Values may be sent and summed in bfloat16 or wider, within the bound.
A program may use at most 64 MiB of HBM per device.

v0:
```python
import jax
import jax.numpy as jnp
from jax import lax
from jax.sharding import PartitionSpec as P

HIGH = lax.Precision.HIGHEST


def from_root(array, axis, root):
    mine = lax.axis_index(axis) == root
    return lax.psum(jnp.where(mine, array, jnp.zeros_like(array)), axis)


def right_solve(factor, rhs):
    return lax.linalg.triangular_solve(factor, rhs, left_side=False, lower=True)


def diag_gradient(factor, lower_part):
    eye = jnp.eye(factor.shape[0], dtype=jnp.float32)
    middle = jnp.dot(factor.T, lower_part, precision=HIGH, preferred_element_type=jnp.float32)
    middle = jnp.tril(middle) - 0.5 * middle * eye
    half = lax.linalg.triangular_solve(factor, middle, left_side=True, lower=True, transpose_a=True)
    full = right_solve(factor, half)
    return full + full.T


def stacked_inner(left, right):
    flat_left = left.reshape(-1, left.shape[-1])
    flat_right = right.reshape(-1, right.shape[-1]).astype(jnp.float32)
    return lax.dot_general(
        flat_left,
        flat_right,
        (((0,), (0,)), ((), ())),
        precision=HIGH,
        preferred_element_type=jnp.float32,
    )


def solve_rows(diag_factor, column, below):
    rows_here, tile = (column.shape[0], column.shape[1])
    inverse = right_solve(diag_factor, jnp.eye(tile, dtype=jnp.float32))
    solved = jnp.dot(
        column.reshape(-1, tile), inverse, precision=HIGH, preferred_element_type=jnp.float32
    ).reshape(rows_here, tile, tile)
    return jnp.where(below, solved, jnp.float32(0.0))


def diag_down(piece, owner_row):
    return from_root(piece, "row", owner_row).astype(jnp.float32)


def per_device(l_saved, l_grad):
    rows_here = l_saved.shape[0]
    tile = l_saved.shape[2]
    n_row = lax.axis_size("row")
    n_col = lax.axis_size("col")
    factor = l_saved.reshape(rows_here, tile, tile)
    grad = l_grad.reshape(rows_here, tile, tile).astype(jnp.float32)
    my_row = lax.axis_index("row")
    my_col = lax.axis_index("col")
    tile_rows = jnp.arange(rows_here, dtype=jnp.int32) * n_row + my_row
    eye = jnp.eye(tile, dtype=jnp.float32)
    for panel in (n_col - 1, n_col - 2):
        owner_row = panel % n_row
        local = panel // n_row
        at_owner = my_row == owner_row
        below = (tile_rows > panel)[:, None, None]
        diag_factor = diag_down(factor[local], owner_row)
        cbar = solve_rows(diag_factor, grad, below)
        term = jnp.where(at_owner, grad[local], jnp.float32(0.0)) - stacked_inner(cbar, factor)
        total = lax.psum(term, "row")
        sym = diag_gradient(diag_factor, jnp.tril(total))
        sent = from_root(jnp.concatenate([cbar, sym[None]], 0), "col", panel)
        cbar = sent[:rows_here]
        sym = sent[rows_here]
        row_factor = from_root(factor[local], "row", owner_row).astype(jnp.float32)
        update = jnp.dot(
            cbar.reshape(-1, tile), row_factor, precision=HIGH, preferred_element_type=jnp.float32
        )
        partial_sum = stacked_inner(cbar, factor)
        summed = lax.psum(partial_sum, "row")
        own_row = grad[local] - (
            summed + jnp.dot(sym, row_factor, precision=HIGH, preferred_element_type=jnp.float32)
        )
        updated = grad - update.reshape(rows_here, tile, tile)
        updated = updated.at[local].set(jnp.where(at_owner, own_row, updated[local]))
        abar = jnp.tril(sym) - 0.5 * sym * eye
        panel_col = jnp.where(
            below,
            cbar,
            jnp.where((tile_rows == panel)[:, None, None], abar[None], jnp.float32(0.0)),
        )
        grad = jnp.where(my_col < panel, updated, jnp.where(my_col == panel, panel_col, grad))
    return grad.reshape(l_grad.shape)


def solution(mesh):
    in_specs = (P(None, "row", None, "col", None), P(None, "row", None, "col", None))
    out_specs = P(None, "row", None, "col", None)
    return jax.shard_map(
        per_device, mesh=mesh, in_specs=in_specs, out_specs=out_specs, check_vma=False
    )
```

profile of v0, /device:TPU:0, one launch (start us, length us, event | category | flops | bytes accessed | tf_op | source)
XLA Modules:
  0.0 607.6 jit_solution(4179768059537039904)
XLA Ops:
  8.3 4.3 convert_element_type.13
  12.6 32.2 %all-reduce.21.cloned.1.call-done = (bf16[256,256]{1,0:T(8,128)(2,1)}, bf16[256,256]{1,0:T(8,128)(2,1)}) async-done(((bf16[256,256]{1,0:T(8,128)(2,1)}, bf16[256,256]{1,0:T(8,128)(2,1)}), (bf16[256,256]{1,0:T(8,128)(2,1)}, bf16[256,256]{1,0:T(8,128)(2,1)})) %all-reduce.21.cloned.1.call-update) | async-done | bytes 262160 | tf_op jit(solution)/shard_map/psum | solution.py:11
  45.9 4.1 while.14
  50.1 19.7 %custom-call.10 = f32[2,128,128]{1,2,0:T(8,128)S(1)} custom-call(f32[2,128,128]{2,1,0:T(8,128)S(1)} %get-tuple-element.71), custom_call_target="InvertDiagBlocksLowerTriangular" | custom-call | tf_op jit(solution)/shard_map/triangular_solve/custom-call.1 | solution.py:15
  70.7 3.8 convolution_bitcast_fusion
  74.6 5.8 copy.9
  80.3 5.0 fusion.5
  85.4 4.7 broadcast_select_fusion
  90.2 27.7 %all-reduce.9.cloned.1.call-done = f32[256,256]{1,0:T(8,128)} async-done(((f32[256,256]{1,0:T(8,128)}), f32[256,256]{1,0:T(8,128)}) %all-reduce.9.cloned.1.call-update) | async-done | bytes 262160 | tf_op jit(solution)/shard_map/psum | solution.py:71
  122.8 4.7 maximum_select_fusion
  127.5 13.2 %all-reduce.13.cloned.1.call-start = ((), (), s32[]{:S(2)}) async-start(), calls=%async_computation.2 | async-start | bytes 524288 | tf_op jit(solution)/shard_map/psum | solution.py:81
  140.7 4.0 while.15
  144.7 19.7 %custom-call.13 = f32[2,128,128]{1,2,0:T(8,128)S(1)} custom-call(f32[2,128,128]{2,1,0:T(8,128)S(1)} %get-tuple-element.74), custom_call_target="InvertDiagBlocksLowerTriangular" | custom-call | tf_op jit(solution)/shard_map/triangular_solve/custom-call.1 | solution.py:15
  165.3 125.3 %all-reduce.11.cloned.1.call-done = f32[17,256,256]{2,1,0:T(8,128)} async-done(((f32[17,256,256]{2,1,0:T(8,128)}), f32[17,256,256]{2,1,0:T(8,128)}) %all-reduce.11.cloned.1.call-update) | async-done | bytes 4456464 | tf_op jit(solution)/shard_map/psum | solution.py:11
  290.7 2.2 slice-done.3
  292.9 4.1 fusion.83
  297.1 4.9 bitcast_subtract_fusion
  305.0 23.4 %all-reduce.13.cloned.1.call-done = f32[256,256]{1,0:T(8,128)} async-done(((f32[256,256]{1,0:T(8,128)}), f32[256,256]{1,0:T(8,128)}) %all-reduce.13.cloned.1.call-update) | async-done | bytes 262160 | tf_op jit(solution)/shard_map/psum | solution.py:81
  328.5 2.1 fusion.12
  330.5 5.1 fusion
  335.7 3.7 convolution_select_fusion
  341.3 4.2 convolution_subtract_fusion.1
  345.6 31.5 %all-reduce.15.cloned.1.call-done = f32[256,256]{1,0:T(8,128)} async-done(((f32[256,256]{1,0:T(8,128)}), f32[256,256]{1,0:T(8,128)}) %all-reduce.15.cloned.1.call-update) | async-done | bytes 262160 | tf_op jit(solution)/shard_map/psum | solution.py:71
  380.3 4.7 maximum_select_fusion.1
  385.3 162.9 %all-reduce.17.cloned.1.call-done = f32[17,256,256]{2,1,0:T(8,128)} async-done(((f32[17,256,256]{2,1,0:T(8,128)}), f32[17,256,256]{2,1,0:T(8,128)}) %all-reduce.17.cloned.1.call-update) | async-done | bytes 4456464 | tf_op jit(solution)/shard_map/psum | solution.py:11
  548.2 2.2 slice-done.2
  550.4 4.1 fusion.84
  554.6 5.6 convolution_subtract_fusion
  562.3 23.7 %all-reduce.19.cloned.1.call-done = f32[256,256]{1,0:T(8,128)} async-done(((f32[256,256]{1,0:T(8,128)}), f32[256,256]{1,0:T(8,128)}) %all-reduce.19.cloned.1.call-update) | async-done | bytes 262160 | tf_op jit(solution)/shard_map/psum | solution.py:81
  586.0 2.1 fusion.15
  588.1 5.9 select_bitcast_fusion
  594.0 6.3 %copy.7 = f32[16,1,256,1,256]{4,3,2,1,0:T(1,128)} copy(f32[16,1,256,1,256]{4,2,0,3,1:T(8,128)S(1)} %select_bitcast_fusion) | data formatting | bytes 8388608 | tf_op jit(solution)/shard_map/reshape | solution.py:94
  (90 shorter events, 28.3 us)
Async XLA Ops:
  6.5 38.3 %all-reduce.21.cloned.1.call-start = ((), (), s32[]{:S(2)}) async-start(), calls=%async_computation.6 | async-start | bytes 524288 | tf_op jit(solution)/shard_map/psum | solution.py:11
  8.2 109.7 %all-reduce.9.cloned.1.call-start = ((), (), s32[]{:S(2)}) async-start(), calls=%async_computation | async-start | bytes 524288 | tf_op jit(solution)/shard_map/psum | solution.py:71
  8.3 62.4 %copy-start.3 = (bf16[16,1,256,1,256]{4,2,3,1,0:T(8,128)(2,1)S(1)}, bf16[16,1,256,1,256]{4,2,3,1,0:T(8,128)(2,1)}, u32[]{:S(2)}) copy-start(bf16[16,1,256,1,256]{4,2,3,1,0:T(8,128)(2,1)} %param.11) | copy-start | bytes 6291460
  74.6 5.8 copy-start.2
  85.4 205.3 %all-reduce.11.cloned.1.call-start = ((), (), s32[]{:S(2)}) async-start(), calls=%async_computation.1 | async-start | bytes 8912896 | tf_op jit(solution)/shard_map/psum | solution.py:11
  85.4 32.4 %copy-start.7 = (bf16[256,256]{1,0:T(8,128)(2,1)S(1)}, bf16[256,256]{1,0:T(8,128)(2,1)}, u32[]{:S(2)}) copy-start(bf16[256,256]{1,0:T(8,128)(2,1)} %get-tuple-element.93) | copy-start | bytes 393220
  127.5 201.0 %all-reduce.13.cloned.1.call-start = ((), (), s32[]{:S(2)}) async-start(), calls=%async_computation.2 | async-start | bytes 524288 | tf_op jit(solution)/shard_map/psum | solution.py:81
  290.7 2.2 slice-start.3
  297.0 80.1 %all-reduce.15.cloned.1.call-start = ((), (), s32[]{:S(2)}) async-start(), calls=%async_computation.3 | async-start | bytes 524288 | tf_op jit(solution)/shard_map/psum | solution.py:71
  302.0 2.0 copy-start.5
  335.6 3.8 copy-start
  339.4 1.9 copy-start.1
  339.4 37.7 %copy-start.6 = (bf16[256,256]{1,0:T(8,128)(2,1)S(1)}, bf16[256,256]{1,0:T(8,128)(2,1)}, u32[]{:S(2)}) copy-start(bf16[256,256]{1,0:T(8,128)(2,1)} %get-tuple-element.94) | copy-start | bytes 393220
  345.5 202.7 %all-reduce.17.cloned.1.call-start = ((), (), s32[]{:S(2)}) async-start(), calls=%async_computation.4 | async-start | bytes 8912896 | tf_op jit(solution)/shard_map/psum | solution.py:11
  385.1 201.0 %all-reduce.19.cloned.1.call-start = ((), (), s32[]{:S(2)}) async-start(), calls=%async_computation.5 | async-start | bytes 524288 | tf_op jit(solution)/shard_map/psum | solution.py:81
  548.2 2.2 slice-start.2
  550.4 11.8 %slice-start = ((s8[4456448]{0:T(1024)(128)(4,1)}), s8[262144]{0:T(1024)(128)(4,1)S(1)}, s32[]{:S(2)}) async-start(s8[4456448]{0:T(1024)(128)(4,1)} %bitcast.165), calls=%async_computation.7 | async-start | bytes 524288
  554.6 7.7 %slice-start.1 = ((s8[4456448]{0:T(1024)(128)(4,1)}), s8[4194304]{0:T(1024)(128)(4,1)S(1)}, s32[]{:S(2)}) async-start(s8[4456448]{0:T(1024)(128)(4,1)} %bitcast.165), calls=%async_computation.8 | async-start | bytes 8388608
  560.2 2.0 copy-start.4
Sparse Core Ops, SparseCore 0:
  9.7 35.0 all-reduce.20
  85.5 32.3 all-reduce.8
  127.6 163.0 all-reduce.10
  297.1 31.2 all-reduce.12
  345.7 31.3 all-reduce.14
  385.2 163.0 all-reduce.16
  554.7 31.2 all-reduce.18
where the time goes:
time: 616 us; the launch traced here: 608 us
  waiting for transfers between devices  427 us (69%)
  other arithmetic  73.2 us (12%)
  matrix products  47.7 us (8%)
  local copies, waits for them, and re-layouts  31.8 us (5%)
  between operations  14.3 us (2%)
  starting transfers between devices  13.6 us (2%)
    psum x3, waiting for transfers between devices, from_root(): return lax.psum(jnp.where(mine, array, jnp.zeros_like(array)), axis)  320 us
    psum x2, waiting for transfers between devices, per_device(): total = lax.psum(term, 'row')  59.2 us
    psum x2, waiting for transfers between devices, per_device(): summed = lax.psum(partial_sum, 'row')  47.1 us
    another operation x6, other arithmetic, right_solve(): return lax.linalg.triangular_solve(factor, rhs, left_side=False, lower=True)  41.1 us
    dot_general x4, matrix products, stacked_inner(): lax.dot_general(flat_left, flat_right, (((0,), (0,)), ((), ())), precisio...  17.4 us
    psum x2, starting transfers between devices, per_device(): summed = lax.psum(partial_sum, 'row')  13.4 us
  transfers between devices with their start and end apart: 7, of which 7 were waited for; matrix products, arithmetic and copies ran while one was open for 7% of the time, Pallas kernels for 0%

commit v1 on v0

--- a/solution.py
+++ b/solution.py
@@ -78,7 +78,9 @@
             cbar.reshape(-1, tile), row_factor, precision=HIGH, preferred_element_type=jnp.float32
         )
         partial_sum = stacked_inner(cbar, factor)
-        summed = lax.psum(partial_sum, "row")
+        summed = partial_sum
+        for hop in (1, 2):
+            summed = summed + lax.ppermute(summed, "row", [(dev, dev ^ hop) for dev in range(4)])
         own_row = grad[local] - (
             summed + jnp.dot(sym, row_factor, precision=HIGH, preferred_element_type=jnp.float32)
         )

time: 616 us -> 564 us (0.916)
  waiting for transfers between devices: 427 us -> 407 us
  matrix products: 47.7 us -> 36.7 us
  starting transfers between devices: 13.6 us -> 3.39 us
  other arithmetic: 73.2 us -> 65.1 us
    psum x2 -> x0, waiting for transfers between devices: 47.1 us -> none  [per_device(): summed = lax.psum(partial_sum, 'row')]
    ppermute x0 -> x4, waiting for transfers between devices: none -> 13.8 us  [per_device(): lax.ppermute(summed, 'row', [(dev, dev ^ hop) for dev in range(4)])]
    psum x2 -> x0, starting transfers between devices: 13.4 us -> none  [per_device(): summed = lax.psum(partial_sum, 'row')]
    psum x3, waiting for transfers between devices: 320 us -> 334 us  [from_root(): return lax.psum(jnp.where(mine, array, jnp.zeros_like(array)), axis)]
    dot_general x2, matrix products: 10.5 us -> 4.3 us  [per_device(): jnp.dot(cbar.reshape(-1, tile), row_factor, precision=HIGH, preferred_ele...]
  transfers between devices with their start and end apart: 7 -> 9, of which waited for: 7 -> 7; matrix products, arithmetic and copies ran while one was open for 7% -> 7% of each run, Pallas kernels for 0% -> 0%
where the time goes in v1:
time: 564 us; the launch traced here: 555 us
  waiting for transfers between devices  407 us (72%)
  other arithmetic  65.1 us (12%)
  matrix products  36.7 us (7%)
  local copies, waits for them, and re-layouts  28.7 us (5%)
  between operations  14 us (2%)
    psum x3, waiting for transfers between devices, from_root(): return lax.psum(jnp.where(mine, array, jnp.zeros_like(array)), axis)  334 us
    psum x2, waiting for transfers between devices, per_device(): total = lax.psum(term, 'row')  59 us
    another operation x6, other arithmetic, right_solve(): return lax.linalg.triangular_solve(factor, rhs, left_side=False, lower=True)  41.3 us
    dot_general x4, matrix products, stacked_inner(): lax.dot_general(flat_left, flat_right, (((0,), (0,)), ((), ())), precisio...  16.3 us
    ppermute x4, waiting for transfers between devices, per_device(): lax.ppermute(summed, 'row', [(dev, dev ^ hop) for dev in range(4)])  13.8 us
  transfers between devices with their start and end apart: 9, of which 7 were waited for; matrix products, arithmetic and copies ran while one was open for 7% of the time, Pallas kernels for 0%

profile of v1, /device:TPU:0, one launch (start us, length us, event | category | flops | bytes accessed | tf_op | source)
XLA Modules:
  0.0 554.8 jit_solution(11825394665499964062)
XLA Ops:
  6.5 1.6 select_bitcast_fusion.1
  8.4 4.3 convert_element_type.13
  12.6 32.2 %all-reduce.15.cloned.1.call-done = (bf16[256,256]{1,0:T(8,128)(2,1)}, bf16[256,256]{1,0:T(8,128)(2,1)}) async-done(((bf16[256,256]{1,0:T(8,128)(2,1)}, bf16[256,256]{1,0:T(8,128)(2,1)}), (bf16[256,256]{1,0:T(8,128)(2,1)}, bf16[256,256]{1,0:T(8,128)(2,1)})) %all-reduce.15.cloned.1.call-update) | async-done | bytes 262160 | tf_op jit(solution)/shard_map/psum | solution.py:11
  45.9 3.8 while.14
  46.5 1.3 bitcast_dynamic-update-slice_fusion.4
  49.8 19.7 %custom-call.10 = f32[2,128,128]{1,2,0:T(8,128)S(1)} custom-call(f32[2,128,128]{2,1,0:T(8,128)S(1)} %get-tuple-element.71), custom_call_target="InvertDiagBlocksLowerTriangular" | custom-call | tf_op jit(solution)/shard_map/triangular_solve/custom-call.1 | solution.py:15
  70.4 3.9 convolution_bitcast_fusion
  74.3 5.7 %copy.9 = f32[4096,256]{1,0:T(8,128)} copy(f32[4096,256]{0,1:T(8,128)} %convolution_bitcast_fusion) | data formatting | bytes 8388608 | tf_op jit(solution)/shard_map/reshape | solution.py:44
  80.1 5.1 fusion.5
  85.2 4.7 broadcast_select_fusion
  89.9 27.6 %all-reduce.7.cloned.1.call-done = f32[256,256]{1,0:T(8,128)} async-done(((f32[256,256]{1,0:T(8,128)}), f32[256,256]{1,0:T(8,128)}) %all-reduce.7.cloned.1.call-update) | async-done | bytes 262160 | tf_op jit(solution)/shard_map/psum | solution.py:71
  122.5 4.7 maximum_select_fusion
  127.3 3.8 while.15
  131.1 19.8 %custom-call.13 = f32[2,128,128]{1,2,0:T(8,128)S(1)} custom-call(f32[2,128,128]{2,1,0:T(8,128)S(1)} %get-tuple-element.74), custom_call_target="InvertDiagBlocksLowerTriangular" | custom-call | tf_op jit(solution)/shard_map/triangular_solve/custom-call.1 | solution.py:15
  151.9 138.5 %all-reduce.9.cloned.1.call-done = f32[17,256,256]{2,1,0:T(8,128)} async-done(((f32[17,256,256]{2,1,0:T(8,128)}), f32[17,256,256]{2,1,0:T(8,128)}) %all-reduce.9.cloned.1.call-update) | async-done | bytes 4456464 | tf_op jit(solution)/shard_map/psum | solution.py:11
  290.4 2.6 slice-done.1
  292.9 3.4 fusion.83
  296.5 2.0 bitcast_subtract_fusion
  298.6 1.5 collective-permute-start.1
  300.4 6.9 %collective-permute-done.1 = f32[256,256]{1,0:T(8,128)S(1)} collective-permute-done((f32[256,256]{1,0:T(8,128)S(1)}, f32[256,256]{1,0:T(8,128)S(1)}, u32[]{:S(2)}, u32[]{:S(2)}) %collective-permute-start.1) | collective-permute-done | bytes 262176 | tf_op jit(solution)/shard_map/ppermute | solution.py:83
  309.6 3.7 convolution_select_fusion
  313.4 2.0 copy-done.4
  315.4 4.4 convolution_subtract_fusion.1
  319.9 31.4 %all-reduce.11.cloned.1.call-done = f32[256,256]{1,0:T(8,128)} async-done(((f32[256,256]{1,0:T(8,128)}), f32[256,256]{1,0:T(8,128)}) %all-reduce.11.cloned.1.call-update) | async-done | bytes 262160 | tf_op jit(solution)/shard_map/psum | solution.py:71
  354.5 4.7 maximum_select_fusion.1
  359.2 163.1 %all-reduce.13.cloned.1.call-done = f32[17,256,256]{2,1,0:T(8,128)} async-done(((f32[17,256,256]{2,1,0:T(8,128)}), f32[17,256,256]{2,1,0:T(8,128)}) %all-reduce.13.cloned.1.call-update) | async-done | bytes 4456464 | tf_op jit(solution)/shard_map/psum | solution.py:11
  522.4 3.1 slice-done
  525.5 3.5 fusion.84
  529.1 2.3 convolution_subtract_fusion
  531.4 1.5 collective-permute-start.3
  533.2 6.9 %collective-permute-done.3 = f32[256,256]{1,0:T(8,128)S(1)} collective-permute-done((f32[256,256]{1,0:T(8,128)S(1)}, f32[256,256]{1,0:T(8,128)S(1)}, u32[]{:S(2)}, u32[]{:S(2)}) %collective-permute-start.3) | collective-permute-done | bytes 262176 | tf_op jit(solution)/shard_map/ppermute | solution.py:83
  541.5 6.3 %copy.7 = f32[16,1,256,1,256]{4,3,2,1,0:T(1,128)} copy(f32[16,1,256,1,256]{4,2,0,3,1:T(8,128)S(1)} %select_bitcast_fusion) | data formatting | bytes 8388608 | tf_op jit(solution)/shard_map/reshape | solution.py:96
  (94 shorter events, 22.2 us)
Async XLA Ops:
  6.5 38.3 %all-reduce.15.cloned.1.call-start = ((), (), s32[]{:S(2)}) async-start(), calls=%async_computation.4 | async-start | bytes 524288 | tf_op jit(solution)/shard_map/psum | solution.py:11
  8.2 109.4 %all-reduce.7.cloned.1.call-start = ((), (), s32[]{:S(2)}) async-start(), calls=%async_computation | async-start | bytes 524288 | tf_op jit(solution)/shard_map/psum | solution.py:71
  8.3 62.1 %copy-start.6 = (bf16[16,1,256,1,256]{4,2,3,1,0:T(8,128)(2,1)S(1)}, bf16[16,1,256,1,256]{4,2,3,1,0:T(8,128)(2,1)}, u32[]{:S(2)}) copy-start(bf16[16,1,256,1,256]{4,2,3,1,0:T(8,128)(2,1)} %param.11) | copy-start | bytes 6291460
  74.3 5.8 %copy-start.5 = (bf16[16,1,256,1,256]{4,2,3,1,0:T(8,128)(2,1)S(1)}, bf16[16,1,256,1,256]{4,2,3,1,0:T(8,128)(2,1)}, u32[]{:S(2)}) copy-start(bf16[16,1,256,1,256]{4,2,3,1,0:T(8,128)(2,1)} %param.10) | copy-start | bytes 6291460
  85.1 205.3 %all-reduce.9.cloned.1.call-start = ((), (), s32[]{:S(2)}) async-start(), calls=%async_computation.1 | async-start | bytes 8912896 | tf_op jit(solution)/shard_map/psum | solution.py:11
  85.2 32.4 %copy-start.9 = (bf16[256,256]{1,0:T(8,128)(2,1)S(1)}, bf16[256,256]{1,0:T(8,128)(2,1)}, u32[]{:S(2)}) copy-start(bf16[256,256]{1,0:T(8,128)(2,1)} %get-tuple-element.93) | copy-start | bytes 393220
  127.2 224.0 %all-reduce.11.cloned.1.call-start = ((), (), s32[]{:S(2)}) async-start(), calls=%async_computation.2 | async-start | bytes 524288 | tf_op jit(solution)/shard_map/psum | solution.py:71
  290.4 2.6 slice-start.1
  290.4 6.1 %copy-start.3 = (f32[17,256,256]{2,1,0:T(8,128)S(1)}, f32[17,256,256]{2,1,0:T(8,128)}, u32[]{:S(2)}) copy-start(f32[17,256,256]{2,1,0:T(8,128)} %all-reduce.9.cloned.1.call-done) | copy-start | bytes 13369348
  290.4 6.1 %copy-start.7 = (bf16[16,1,256,1,256]{4,2,3,1,0:T(8,128)(2,1)S(1)}, bf16[16,1,256,1,256]{4,2,3,1,0:T(8,128)(2,1)}, u32[]{:S(2)}) copy-start(bf16[16,1,256,1,256]{4,2,3,1,0:T(8,128)(2,1)} %param.11) | copy-start | bytes 6291460
  296.4 2.1 collective-permute-start
  298.6 8.8 %collective-permute-start.1 = (f32[256,256]{1,0:T(8,128)S(1)}, f32[256,256]{1,0:T(8,128)S(1)}, u32[]{:S(2)}, u32[]{:S(2)}) collective-permute-start(f32[256,256]{1,0:T(8,128)S(1)} %add.66), channel_id=1, source_target_pairs={{0,16},{8,24},{16,0},{24,8},{1,17},{9,25},{17,1},{25,9},{2,18},{10... | collective-permute-start | bytes 786440 | tf_op jit(solution)/shard_map/ppermute | solution.py:83
  309.6 3.8 copy-start
  313.4 2.0 copy-start.4
  313.4 37.9 %copy-start.8 = (bf16[256,256]{1,0:T(8,128)(2,1)S(1)}, bf16[256,256]{1,0:T(8,128)(2,1)}, u32[]{:S(2)}) copy-start(bf16[256,256]{1,0:T(8,128)(2,1)} %get-tuple-element.94) | copy-start | bytes 393220
  319.8 202.6 %all-reduce.13.cloned.1.call-start = ((), (), s32[]{:S(2)}) async-start(), calls=%async_computation.3 | async-start | bytes 8912896 | tf_op jit(solution)/shard_map/psum | solution.py:11
  522.4 3.1 slice-start
  522.4 6.7 %copy-start.2 = (f32[17,256,256]{2,1,0:T(8,128)S(1)}, f32[17,256,256]{2,1,0:T(8,128)}, u32[]{:S(2)}) copy-start(f32[17,256,256]{2,1,0:T(8,128)} %all-reduce.13.cloned.1.call-done) | copy-start | bytes 13369348
  522.4 6.7 %copy-start.1 = (f32[16,256,256]{2,1,0:T(8,128)S(1)}, f32[16,256,256]{2,1,0:T(8,128)}, u32[]{:S(2)}) copy-start(f32[16,256,256]{2,1,0:T(8,128)} %copy-done) | copy-start | bytes 12582916
  529.0 2.4 collective-permute-start.2
  531.4 8.8 %collective-permute-start.3 = (f32[256,256]{1,0:T(8,128)S(1)}, f32[256,256]{1,0:T(8,128)S(1)}, u32[]{:S(2)}, u32[]{:S(2)}) collective-permute-start(f32[256,256]{1,0:T(8,128)S(1)} %add.70), channel_id=1, source_target_pairs={{0,16},{8,24},{16,0},{24,8},{1,17},{9,25},{17,1},{25,9},{2,18},{10... | collective-permute-start | bytes 786440 | tf_op jit(solution)/shard_map/ppermute | solution.py:83
Sparse Core Ops, SparseCore 0:
  9.7 35.0 all-reduce.14
  85.2 32.2 all-reduce.6
  127.3 163.0 all-reduce.8
  319.9 31.2 all-reduce.10
  359.3 162.9 all-reduce.12
